TPU v7x, 256 devices: a whole 4x4x8 slice. The times are simulated.
256 devices in a mesh: samp: 4 (over y), snp: 64 (over z, x, core).
Axes of the slice: x: 4, y: 4, z: 8, core: 2. Of those that a mesh axis runs over, the one named last changes fastest.
Arguments:
- genotypes: int32 [8192, 65536], P('samp', 'snp'), may hold values from 0 to 2
- win_lo: int32 [65536], P('snp'), may hold values from 0 to 65535, as said below
- win_hi: int32 [65536], P('snp'), may hold values from 0 to 65535, as said below
- annotation: int32 [65536], P('snp'), may hold values from 0 to 127
- chromosome: int32 [65536], P('snp'), may hold values from 0 to 21, never falling along the last dimension, each value on 1 to 4096 neighbouring positions
- chi_square: float32 [65536], P('snp'), may hold values from 0.3 to 60
Outputs:
- annotation_scores: float32 [128, 65536], P('snp')
- gram: float32 [128, 128], replicated
- moments: float32 [2, 128], replicated
- totals: float32 [2], replicated
Inputs may be any that keep to these rules, and one draw needn't show every extreme that they name: i - 512 <= win_lo[i] <= i, nondecreasing in i; the distance 512 is reached. i <= win_hi[i] <= i + 512, nondecreasing in i; the distance 512 is reached.
All inputs are finite; a program needn't handle non-finite values.
Results may differ from a plain program's by a relative error of at most 0.0003.
The roundings to bfloat16 on the way count: a program that leaves them out, or rounds other values in their place, can miss the bound.
Values may be sent and summed in bfloat16 or wider, within the bound.
No kernel may reach another device: no remote copies, remote signals or barrier semaphores. Data moves between devices by JAX's collectives and lax.ppermute only.
A program may use at most 64 MiB of HBM per device.

v0:
```python
import jax
import jax.numpy as jnp
from jax import lax
from jax.sharding import PartitionSpec as P

A = 128


def from_everyone(array, axis):
    size = lax.axis_size(axis)
    return lax.all_to_all(
        jnp.broadcast_to(array[None], (size, *array.shape)), axis, 0, 0, tiled=True
    )


def of_everyone(array, axis):
    return from_everyone(array, axis).sum(axis=0)


def packed_total(arrays, axis):
    flat, at, finished = (jnp.concatenate([a.reshape(-1) for a in arrays]), 0, [])
    so_far = of_everyone(flat, axis)
    for a in arrays:
        finished.append(so_far[at : at + a.size].reshape(a.shape))
        at += a.size
    return tuple(finished)


def extended(cells, sides, width):
    for axis, dim in sides:
        count = lax.axis_size(axis)
        ends = count - 1
        head = lax.slice_in_dim(cells, 0, width, axis=dim)
        tail = lax.slice_in_dim(cells, cells.shape[dim] - width, cells.shape[dim], axis=dim)
        cells = jnp.concatenate(
            [
                lax.ppermute(tail, axis, [(i, (i + 1) % count) for i in range(ends)]),
                cells,
                lax.ppermute(head, axis, [((i + 1) % count, i) for i in range(ends)]),
            ],
            axis=dim,
        )
    return cells


def cut_along(array, dim, size):
    dims = array.shape
    pieces = array.reshape(*dims[:dim], size, dims[dim] // size, *dims[dim + 1 :])
    return jnp.moveaxis(pieces, dim, 0)


def sum_at_owner(array, axis, dim):
    pieces = cut_along(array, dim, lax.axis_size(axis))
    arrived = lax.all_to_all(pieces, axis, split_axis=0, concat_axis=0, tiled=True)
    return arrived.sum(axis=0)


def rows_for(lines, size):
    spare = -lines.shape[0] % size
    if not spare:
        return lines
    return jnp.concatenate([lines, jnp.zeros((spare, *lines.shape[1:]), lines.dtype)])


def laid_out(pieces, dim):
    dims = list(pieces.shape[1:])
    dims[dim] *= pieces.shape[0]
    return jnp.moveaxis(pieces, 0, dim).reshape(dims)


def collect(array, axis, dim):
    pieces = from_everyone(array, axis)
    return laid_out(pieces, dim)


def total_of(array, axes):
    own = sum_at_owner(rows_for(array, lax.axis_size(axes)), axes, 0)
    whole = collect(own, axes, 0)
    return whole[: len(array)].reshape(array.shape)


def in_one(arrays, axis):
    ends = [0]
    for a in arrays:
        ends.append(ends[-1] + a.size)
    so_far = total_of(jnp.concatenate([a.ravel() for a in arrays]), axis)
    return tuple((so_far[b:e].reshape(a.shape) for a, b, e in zip(arrays, ends, ends[1:])))


def body(genotypes, win_lo, win_hi, annotation, chromosome, chi_square):
    samp_rows, block_cols = genotypes.shape
    reach = block_cols // 2
    samp_count = lax.axis_size("samp")
    total_samples = samp_rows * samp_count
    dosage = genotypes.astype(jnp.float32)
    dose_sums, dose_squares = packed_total(
        (jnp.sum(dosage, 0), jnp.sum(dosage * dosage, 0)), "samp"
    )
    mean_dose = dose_sums / total_samples
    variance = dose_squares / total_samples - mean_dose * mean_dose
    standard = ((dosage - mean_dose) * lax.rsqrt(variance + 1e-05)).astype(jnp.bfloat16)
    first_snp = lax.axis_index("snp") * block_cols
    labels = jnp.arange(A, dtype=jnp.int32)
    own_labels = jnp.stack([annotation, chromosome]).astype(jnp.bfloat16)
    wide_z, wide_labels = (
        extended(standard, (("snp", 1),), reach),
        extended(own_labels, (("snp", 1),), reach),
    )
    annot_wide = wide_labels[0].astype(jnp.int32)
    chrom_wide = wide_labels[1].astype(jnp.int32)
    span = wide_z.shape[1] - block_cols + reach

    def tile_piece(row_start, count):
        band = row_start // reach * reach
        rows_z = lax.dynamic_slice_in_dim(standard, row_start, count, 1)
        cols_z = lax.dynamic_slice_in_dim(wide_z, band, span, 1)
        return lax.dot_general(
            rows_z, cols_z, (((0,), (0,)), ((), ())), preferred_element_type=jnp.float32
        )

    share = block_cols // samp_count
    row_start = jnp.int32(0)
    tile = sum_at_owner(
        jnp.concatenate(
            [
                tile_piece(row_start + offset * share, share)
                for offset in range(share * lax.axis_size("samp") // share)
            ],
            0,
        ),
        "samp",
        0,
    )
    row_begin = lax.axis_index("samp") * share
    row_start = row_begin + 0
    band = row_start // reach * reach
    corr = tile / total_samples
    square = corr * corr
    adjusted = square - (1.0 - square) / (total_samples - 2)
    col_ids = first_snp + band - reach + jnp.arange(span, dtype=jnp.int32)
    lower_end = lax.dynamic_slice_in_dim(win_lo, row_start, share)
    upper_end = lax.dynamic_slice_in_dim(win_hi, row_start, share)
    chrom_rows = lax.dynamic_slice_in_dim(chromosome, row_start, share)
    chrom_cols = lax.dynamic_slice_in_dim(chrom_wide, band, span)
    annot_cols = lax.dynamic_slice_in_dim(annot_wide, band, span)
    inside = (col_ids[None, :] >= lower_end[:, None]) & (col_ids[None, :] <= upper_end[:, None])
    inside = inside & (chrom_cols[None, :] == chrom_rows[:, None])
    kept = jnp.where(inside, adjusted, 0.0)
    member = (annot_cols[:, None] == labels[None, :]).astype(jnp.float32)
    part_scores = lax.dot_general(
        member,
        kept,
        (((0,), (1,)), ((), ())),
        precision=lax.Precision.HIGHEST,
        preferred_element_type=jnp.float32,
    )
    scores = lax.all_gather(part_scores, "samp", axis=1, tiled=True)
    weights = 1.0 / jnp.sum(scores, 0)
    weighted = scores * weights[None, :]
    gram_part = lax.dot_general(
        weighted,
        scores,
        (((1,), (1,)), ((), ())),
        precision=lax.Precision.HIGHEST,
        preferred_element_type=jnp.float32,
    )
    moment_part = jnp.stack([jnp.sum(weighted, 1), jnp.sum(weighted * chi_square[None, :], 1)])
    total_part = jnp.stack([jnp.sum(weights), jnp.sum(weights * chi_square)])
    gram, moments, totals = in_one((gram_part, moment_part, total_part), "snp")
    snp_total = block_cols * lax.axis_size("snp")
    scale = A / snp_total
    regrouped = lax.all_to_all(scores, "snp", split_axis=0, concat_axis=1, tiled=True)
    return (regrouped, scale * gram, scale * moments, totals / snp_total)


def solution(mesh):
    in_specs = (P("samp", "snp"), P("snp"), P("snp"), P("snp"), P("snp"), P("snp"))
    out_specs = (P("snp", None), P(), P(), P())
    return jax.shard_map(body, mesh=mesh, in_specs=in_specs, out_specs=out_specs, check_vma=False)
```

profile of v0, /device:TPU:1, one launch (start us, length us, event | category | flops | bytes accessed | tf_op | source)
XLA Modules:
  0.0 217.3 jit_solution(6880136489920575053)
XLA Ops:
  0.6 4.5 %convert_reduce_fusion = (f32[1024]{0:T(1024)S(1)}, f32[1024]{0:T(1024)S(1)}) fusion(s32[2048,1024]{1,0:T(8,128)} %param.6), kind=kLoop, calls=%fused_computation.2 | loop fusion | flops 8386560 | bytes 8396800 | tf_op jit(solution)/shard_map/reduce_sum | solution.py:97
  5.2 9.1 %all_to_all.45 = f32[4,1,2048]{2,1,0:T(1,128)S(1)} all-to-all(f32[4,1,2048]{2,1,0:T(1,128)S(1)} %broadcast_in_dim.9), channel_id=1, replica_groups=mesh['samp'=4,'snp'=64] {'samp'}, dimensions={0} | all-to-all | bytes 65536 | tf_op jit(solution)/shard_map/all_to_all | solution.py:11
  14.4 4.7 %multiply_convert_fusion = bf16[2048,1024]{1,0:T(8,128)(2,1)S(1)} fusion(s32[2048,1024]{1,0:T(8,128)} %param.6, f32[1024]{0:T(1024)S(1)} %get-tuple-element.17, f32[1024]{0:T(1024)S(1)} %get-tuple-element.16), kind=kLoop, calls=%fused_computation | loop fusion | flops 8388608 | bytes 12591104 | tf_op jit(solution)/shard_map/convert_element_type | solution.py:101
  19.4 4.0 %collective-permute-start.3 = (bf16[2048,512]{1,0:T(8,128)(2,1)S(1)}, bf16[2048,512]{1,0:T(8,128)(2,1)S(1)}, u32[]{:S(2)}, u32[]{:S(2)}) collective-permute-start(bf16[2048,512]{1,0:T(8,128)(2,1)S(1)} %get-tuple-element.11), channel_id=1, source_target_pairs={{1,0},{2,1},{3,2},{4,3},{5,4},{6,5},{7,6},{8,7},{9,8},{10,9},{11,1... | collective-permute-start | bytes 6291464 | tf_op jit(solution)/shard_map/ppermute | solution.py:39
  23.4 3.0 %collective-permute-start.2 = (bf16[2048,512]{1,0:T(8,128)(2,1)S(1)}, bf16[2048,512]{1,0:T(8,128)(2,1)S(1)}, u32[]{:S(2)}, u32[]{:S(2)}) collective-permute-start(bf16[2048,512]{1,0:T(8,128)(2,1)S(1)} %get-tuple-element.10), channel_id=1, source_target_pairs={{0,1},{1,2},{2,3},{3,4},{4,5},{5,6},{6,7},{7,8},{8,9},{9,10},{10,1... | collective-permute-start | bytes 6291464 | tf_op jit(solution)/shard_map/ppermute | solution.py:37
  26.4 22.2 %collective-permute-done.3 = bf16[2048,512]{1,0:T(8,128)(2,1)S(1)} collective-permute-done((bf16[2048,512]{1,0:T(8,128)(2,1)S(1)}, bf16[2048,512]{1,0:T(8,128)(2,1)S(1)}, u32[]{:S(2)}, u32[]{:S(2)}) %collective-permute-start.3) | collective-permute-done | bytes 2097184 | tf_op jit(solution)/shard_map/ppermute | solution.py:39
  48.6 1.8 fusion
  50.4 1.8 fusion.1
  52.2 1.8 fusion.2
  54.0 1.8 fusion.3
  55.9 3.0 %pad_maximum_fusion.2 = f32[1024,1536]{1,0:T(8,128)} fusion(f32[256,1536]{1,0:T(8,128)S(1)} %fusion, f32[256,1536]{1,0:T(8,128)S(1)} %fusion.1, f32[256,1536]{1,0:T(8,128)S(1)} %fusion.2, f32[256,1536]{1,0:T(8,128)S(1)} %fusion.3), kind=kLoop, calls=%fused_computation.5 | loop fusion | flops 4718592 | bytes 12582912 | tf_op jit(solution)/shard_map/concatenate | solution.py:124
  58.9 5.4 %all-to-all-start.1 = ((f32[4,256,1536]{2,1,0:T(8,128)}), f32[4,256,1536]{2,1,0:T(8,128)}, u32[]{:S(2)}, u32[]{:S(2)}) async-start(f32[4,256,1536]{2,1,0:T(8,128)} %bitcast.17), calls=%async_computation.1 | async-start | bytes 12582912 | tf_op jit(solution)/shard_map/all_to_all | solution.py:54
  64.3 1.9 collective-permute-start.1
  66.3 3.8 %collective-permute-start = (bf16[2,512]{1,0:T(2,128)(2,1)S(1)}, bf16[2,512]{1,0:T(2,128)(2,1)S(1)}, u32[]{:S(2)}, u32[]{:S(2)}) collective-permute-start(bf16[2,512]{1,0:T(2,128)(2,1)S(1)} %get-tuple-element.14), channel_id=1, source_target_pairs={{0,1},{1,2},{2,3},{3,4},{4,5},{5,6},{6,7},{7,8},{8,9},{9,10},{10,1... | collective-permute-start | bytes 6152 | tf_op jit(solution)/shard_map/ppermute | solution.py:37
  71.8 44.8 %all-to-all-done.1 = f32[4,256,1536]{2,1,0:T(8,128)} async-done(((f32[4,256,1536]{2,1,0:T(8,128)}), f32[4,256,1536]{2,1,0:T(8,128)}, u32[]{:S(2)}, u32[]{:S(2)}) %all-to-all-start.1) | async-done | bytes 6291488 | tf_op jit(solution)/shard_map/all_to_all | solution.py:54
  116.7 3.6 %reduce_sum.93 = f32[256,1536]{1,0:T(8,128)S(1)} reduce(f32[4,256,1536]{2,1,0:T(8,128)} %all-to-all-done.1, f32[]{:T(128)} %constant.123.clone.1), dimensions={0}, to_apply=%region_3.4 | reduce | flops 1179648 | bytes 7864324 | tf_op jit(solution)/shard_map/reduce_sum | solution.py:55
  120.2 1.6 fusion.4
  121.9 9.9 %all_gather.3 = f32[128,1024]{1,0:T(8,128)S(1)} all-gather(f32[128,256]{1,0:T(8,128)S(1)} %fusion.4), channel_id=1, replica_groups=mesh['samp'=4,'snp'=64] {'samp'}, dimensions={1}, use_global_device_ids=true | all-gather | bytes 655360 | tf_op jit(solution)/shard_map/all_gather | solution.py:157
  133.2 1.4 concatenate.24
  134.9 43.4 %all_to_all.46 = f32[64,1,261]{2,1,0:T(1,128)S(1)} all-to-all(f32[64,1,261]{2,1,0:T(1,128)S(1)} %all_to_all.37), channel_id=1, replica_groups=mesh['samp'=4,'snp'=64] {'snp'}, dimensions={0} | all-to-all | bytes 133632 | tf_op jit(solution)/shard_map/all_to_all | solution.py:54
  179.0 4.4 %all-to-all-start.4 = ((f32[64,1,261]{2,1,0:T(1,128)}), f32[64,1,261]{2,1,0:T(1,128)S(1)}, u32[]{:S(2)}, u32[]{:S(2)}) async-start(f32[64,1,261]{2,1,0:T(1,128)} %broadcast_in_dim.12), calls=%async_computation.4 | async-start | bytes 196608 | tf_op jit(solution)/shard_map/all_to_all | solution.py:11
  184.6 9.6 %all-to-all-done.4 = f32[64,1,261]{2,1,0:T(1,128)S(1)} async-done(((f32[64,1,261]{2,1,0:T(1,128)}), f32[64,1,261]{2,1,0:T(1,128)S(1)}, u32[]{:S(2)}, u32[]{:S(2)}) %all-to-all-start.4) | async-done | bytes 66848 | tf_op jit(solution)/shard_map/all_to_all | solution.py:11
  194.2 4.5 %all-to-all-start.2 = ((f32[64,2,1024]{2,1,0:T(2,128)}), f32[64,2,1024]{2,1,0:T(2,128)S(1)}, u32[]{:S(2)}, u32[]{:S(2)}) async-start(f32[64,2,1024]{2,1,0:T(2,128)} %all_to_all.33), calls=%async_computation.2 | async-start | bytes 1048576 | tf_op jit(solution)/shard_map/all_to_all | solution.py:172
  200.8 15.6 %all-to-all-done.2 = f32[64,2,1024]{2,1,0:T(2,128)S(1)} async-done(((f32[64,2,1024]{2,1,0:T(2,128)}), f32[64,2,1024]{2,1,0:T(2,128)S(1)}, u32[]{:S(2)}, u32[]{:S(2)}) %all-to-all-start.2) | async-done | bytes 524320 | tf_op jit(solution)/shard_map/all_to_all | solution.py:172
  (42 shorter events, 8.6 us)
Async XLA Ops:
  19.4 29.2 %collective-permute-start.3 = (bf16[2048,512]{1,0:T(8,128)(2,1)S(1)}, bf16[2048,512]{1,0:T(8,128)(2,1)S(1)}, u32[]{:S(2)}, u32[]{:S(2)}) collective-permute-start(bf16[2048,512]{1,0:T(8,128)(2,1)S(1)} %get-tuple-element.11), channel_id=1, source_target_pairs={{1,0},{2,1},{3,2},{4,3},{5,4},{6,5},{7,6},{8,7},{9,8},{10,9},{11,1... | collective-permute-start | bytes 6291464 | tf_op jit(solution)/shard_map/ppermute | solution.py:39
  23.4 28.8 %collective-permute-start.2 = (bf16[2048,512]{1,0:T(8,128)(2,1)S(1)}, bf16[2048,512]{1,0:T(8,128)(2,1)S(1)}, u32[]{:S(2)}, u32[]{:S(2)}) collective-permute-start(bf16[2048,512]{1,0:T(8,128)(2,1)S(1)} %get-tuple-element.10), channel_id=1, source_target_pairs={{0,1},{1,2},{2,3},{3,4},{4,5},{5,6},{6,7},{7,8},{8,9},{9,10},{10,1... | collective-permute-start | bytes 6291464 | tf_op jit(solution)/shard_map/ppermute | solution.py:37
  58.9 5.4 %copy-start.2 = (s32[1024]{0:T(1024)S(1)}, s32[1024]{0:T(1024)}, u32[]{:S(2)}) copy-start(s32[1024]{0:T(1024)} %param.9) | copy-start | bytes 12292
  58.9 5.4 %copy-start.1 = (s32[1024]{0:T(1024)S(1)}, s32[1024]{0:T(1024)}, u32[]{:S(2)}) copy-start(s32[1024]{0:T(1024)} %param.10) | copy-start | bytes 12292
  58.9 57.8 %all-to-all-start.1 = ((f32[4,256,1536]{2,1,0:T(8,128)}), f32[4,256,1536]{2,1,0:T(8,128)}, u32[]{:S(2)}, u32[]{:S(2)}) async-start(f32[4,256,1536]{2,1,0:T(8,128)} %bitcast.17), calls=%async_computation.1 | async-start | bytes 12582912 | tf_op jit(solution)/shard_map/all_to_all | solution.py:54
  64.3 7.4 %collective-permute-start.1 = (bf16[2,512]{1,0:T(2,128)(2,1)S(1)}, bf16[2,512]{1,0:T(2,128)(2,1)S(1)}, u32[]{:S(2)}, u32[]{:S(2)}) collective-permute-start(bf16[2,512]{1,0:T(2,128)(2,1)S(1)} %get-tuple-element.15), channel_id=1, source_target_pairs={{1,0},{2,1},{3,2},{4,3},{5,4},{6,5},{7,6},{8,7},{9,8},{10,9},{11,1... | collective-permute-start | bytes 6152 | tf_op jit(solution)/shard_map/ppermute | solution.py:39
  66.3 5.5 %collective-permute-start = (bf16[2,512]{1,0:T(2,128)(2,1)S(1)}, bf16[2,512]{1,0:T(2,128)(2,1)S(1)}, u32[]{:S(2)}, u32[]{:S(2)}) collective-permute-start(bf16[2,512]{1,0:T(2,128)(2,1)S(1)} %get-tuple-element.14), channel_id=1, source_target_pairs={{0,1},{1,2},{2,3},{3,4},{4,5},{5,6},{6,7},{7,8},{8,9},{9,10},{10,1... | collective-permute-start | bytes 6152 | tf_op jit(solution)/shard_map/ppermute | solution.py:37
  120.2 11.6 %copy-start = (f32[1024]{0:T(1024)S(1)}, f32[1024]{0:T(1024)}, u32[]{:S(2)}) copy-start(f32[1024]{0:T(1024)} %param.11) | copy-start | bytes 12292
  179.0 15.2 %all-to-all-start.4 = ((f32[64,1,261]{2,1,0:T(1,128)}), f32[64,1,261]{2,1,0:T(1,128)S(1)}, u32[]{:S(2)}, u32[]{:S(2)}) async-start(f32[64,1,261]{2,1,0:T(1,128)} %broadcast_in_dim.12), calls=%async_computation.4 | async-start | bytes 196608 | tf_op jit(solution)/shard_map/all_to_all | solution.py:11
  194.2 22.3 %all-to-all-start.2 = ((f32[64,2,1024]{2,1,0:T(2,128)}), f32[64,2,1024]{2,1,0:T(2,128)S(1)}, u32[]{:S(2)}, u32[]{:S(2)}) async-start(f32[64,2,1024]{2,1,0:T(2,128)} %all_to_all.33), calls=%async_computation.2 | async-start | bytes 1048576 | tf_op jit(solution)/shard_map/all_to_all | solution.py:172
where the time goes:
time: 218 us; the launch traced here: 217 us
  waiting for transfers between devices  92.3 us (42%)
  blocking collectives  62.4 us (29%)
  starting transfers between devices  27 us (12%)
  other arithmetic  18.8 us (9%)
  matrix products  9.47 us (4%)
  local copies, waits for them, and re-layouts  6.39 us (3%)
    all_to_all x1, waiting for transfers between devices, sum_at_owner(): lax.all_to_all(pieces, axis, split_axis=0, concat_axis=0, tiled=True)  44.8 us
    all_to_all x1, blocking collectives, sum_at_owner(): lax.all_to_all(pieces, axis, split_axis=0, concat_axis=0, tiled=True)  43.4 us
    ppermute x2, waiting for transfers between devices, extended(): lax.ppermute(head, axis, [((i + 1) % count, i) for i in range(ends)])  22.2 us
    all_to_all x1, waiting for transfers between devices, body(): lax.all_to_all(scores, 'snp', split_axis=0, concat_axis=1, tiled=True)  15.6 us
    all_gather x1, blocking collectives, body(): scores = lax.all_gather(part_scores, 'samp', axis=1, tiled=True)  9.9 us
    all_to_all x1, waiting for transfers between devices, from_everyone(): lax.all_to_all(jnp.broadcast_to(array[None], (size, *array.shape)), axis,...  9.6 us
    all_to_all x1, blocking collectives, from_everyone(): lax.all_to_all(jnp.broadcast_to(array[None], (size, *array.shape)), axis,...  9.1 us
    dot_general x4, matrix products, tile_piece(): lax.dot_general(rows_z, cols_z, (((0,), (0,)), ((), ())), preferred_eleme...  7.24 us
  transfers between devices with their start and end apart: 7, of which 4 were waited for; matrix products, arithmetic and copies ran while one was open for 3% of the time, Pallas kernels for 0%

commit v1 on v0

v1 whole, which is shorter than its diff:
```python
import functools

import jax
import jax.numpy as jnp
from jax import lax
from jax.experimental import pallas as pl
from jax.experimental.pallas import tpu as pltpu
from jax.sharding import PartitionSpec as P

A = 128
FIXED = 32000.0


def exchange(array, axis):
    return lax.all_to_all(array, axis, 0, 0, tiled=True)


def to_all(array, axis):
    size = lax.axis_size(axis)
    return exchange(jnp.broadcast_to(array[None], (size, *array.shape)), axis)


def shifted(array, axis, step):
    size = lax.axis_size(axis)
    return lax.ppermute(array, axis, [(i, (i + step) % size) for i in range(size)])


def samp_total(array):
    near, far, back = [shifted(array, "samp", step) for step in (1, 2, 3)]
    return (array + far) + (near + back)


def from_left(array, axis):
    count = lax.axis_size(axis)
    return lax.ppermute(array, axis, [(i, i + 1) for i in range(count - 1)])


def from_right(array, axis):
    count = lax.axis_size(axis)
    return lax.ppermute(array, axis, [(i + 1, i) for i in range(count - 1)])


def gram_of(rows, cols):
    return lax.dot_general(rows, cols, (((0,), (0,)), ((), ())), preferred_element_type=jnp.float32)


def count_kernel(genotypes, lower, upper, sums, held, arrived):
    rows, cols = genotypes.shape
    slots, step, _ = held.shape
    half = cols // 2
    steps = rows // step

    def load(index):
        return pltpu.make_async_copy(
            genotypes.at[pl.ds(index * step, step), :],
            held.at[index % slots],
            arrived.at[index % slots],
        )

    for index in range(slots):
        load(index).start()
    plain = jnp.zeros((8, cols), jnp.float32)
    squared = jnp.zeros((8, cols), jnp.float32)
    for index in range(steps):
        load(index).wait()
        wide = held[index % slots].astype(jnp.float32)
        narrow = wide.astype(jnp.bfloat16)
        lower[index * step : (index + 1) * step, :] = narrow[:, :half]
        upper[index * step : (index + 1) * step, :] = narrow[:, half:]
        folded = wide.reshape(step // 8, 8, cols)
        plain += jnp.sum(folded, 0)
        squared += jnp.sum(folded * folded, 0)
        if index + slots < steps:
            load(index + slots).start()
    sums[0:1, :] = jnp.sum(plain, 0, keepdims=True)
    sums[1:2, :] = jnp.sum(squared, 0, keepdims=True)


def counted(genotypes):
    rows, cols = genotypes.shape
    step = rows // 16
    half = jax.ShapeDtypeStruct((rows, cols // 2), jnp.bfloat16)
    return pl.pallas_call(
        count_kernel,
        out_shape=(half, half, jax.ShapeDtypeStruct((2, cols), jnp.float32)),
        in_specs=[pl.BlockSpec(memory_space=pl.ANY)],
        out_specs=(pl.BlockSpec(memory_space=pltpu.VMEM),) * 3,
        scratch_shapes=[pltpu.VMEM((4, step, cols), jnp.int32), pltpu.SemaphoreType.DMA((4,))],
        compiler_params=pltpu.CompilerParams(vmem_limit_bytes=57 * 2**20),
        name="counted",
    )(genotypes)


def score_kernel(total_samples, *refs):
    near, far, noted, bounds, out = refs[:4], refs[4:8], refs[8:11], refs[11:14], refs[14]
    share, reach = near[0].shape[0] // 3, near[0].shape[1]
    me = lax.axis_index("samp")
    first = lax.axis_index("snp") * (2 * reach)
    blocks = reach // share

    def summed(parts, begin, size):
        held = [part[begin : begin + size, :].astype(jnp.int32) for part in parts]
        return (held[0] + held[1] + held[2] + held[3]).astype(jnp.float32) * (1.0 / FIXED)

    def column(row):
        return jnp.transpose(jnp.broadcast_to(row, (share, share)))[:, 0:1]

    row_id = lax.broadcasted_iota(jnp.int32, (share, reach), 0) + me * share
    col_id = lax.broadcasted_iota(jnp.int32, (share, reach), 1)
    own_0, own_1 = summed(near, 0, share), summed(near, share, share)
    mixed, outer = summed(near, 2 * share, share), summed(far, 0, share)
    edge = column(summed(far, share, 8)[0:1, :share])
    outer_1 = jnp.where(row_id == col_id, edge, outer)
    cat_id = lax.broadcasted_iota(jnp.int32, (A, reach), 0).astype(jnp.float32)
    left, here, right = noted
    sides = [
        (left[0:1, :], left[1:2, :]),
        (here[0:1, :reach], here[1:2, :reach]),
        (here[0:1, reach:], here[1:2, reach:]),
        (right[0:1, :], right[1:2, :]),
    ]
    members = [(annot == cat_id).astype(jnp.bfloat16) for annot, _ in sides]
    scores, chis = [], []
    for half, parts in enumerate(((outer, own_0, mixed), (mixed, own_1, outer_1))):
        at = half * blocks + me
        low, high = [column(ref[pl.ds(at, 1), :]) for ref in bounds[:2]]
        chis.append(bounds[2][pl.ds(at, 1), :])
        start = pl.multiple_of(half * reach + me * share, share)
        chrom = column(here[1:2, pl.ds(start, share)])
        total = jnp.zeros((A, share), jnp.float32)
        for side, corr in enumerate(parts, half):
            square = corr * corr
            adjusted = square - (1.0 - square) / (total_samples - 2)
            ids = first + (side - 1) * reach + col_id
            inside = (ids >= low) & (ids <= high) & (sides[side][1] == chrom)
            rest = jnp.where(inside, adjusted, 0.0)
            for _ in range(3):
                piece = rest.astype(jnp.bfloat16)
                rest = rest - piece.astype(jnp.float32)
                total += lax.dot_general(
                    members[side],
                    piece,
                    (((1,), (1,)), ((), ())),
                    preferred_element_type=jnp.float32,
                )
        scores.append(total)
    score = jnp.concatenate(scores, 1)
    chi = jnp.concatenate(chis, 1)
    weights = 1.0 / jnp.sum(score, 0, keepdims=True)
    weighted = score * weights
    out[:, : 2 * share] = score
    out[:, 2 * share : 2 * share + A] = lax.dot_general(
        weighted,
        score,
        (((1,), (1,)), ((), ())),
        precision=lax.Precision.HIGHEST,
        preferred_element_type=jnp.float32,
    )
    lane = lax.broadcasted_iota(jnp.int32, (A, A), 1)
    plain = jnp.sum(weighted, 1, keepdims=True)
    scaled = jnp.sum(weighted * chi, 1, keepdims=True)
    all_weights = jnp.sum(weights, 1, keepdims=True)
    all_scaled = jnp.sum(weights * chi, 1, keepdims=True)
    out[:, 2 * share + A :] = jnp.where(
        lane == 0,
        plain,
        jnp.where(
            lane == 1,
            scaled,
            jnp.where(lane == 2, all_weights, jnp.where(lane == 3, all_scaled, 0.0)),
        ),
    )


def scored(near, far, noted, bounds, total_samples):
    share = near[0].shape[0] // 3
    operands = [*near, *far, *noted, *bounds]
    return pl.pallas_call(
        functools.partial(score_kernel, total_samples),
        out_shape=jax.ShapeDtypeStruct((A, 2 * share + 2 * A), jnp.float32),
        in_specs=[pl.BlockSpec(memory_space=pltpu.VMEM)] * len(operands),
        out_specs=pl.BlockSpec(memory_space=pltpu.VMEM),
        compiler_params=pltpu.CompilerParams(vmem_limit_bytes=16 * 2**20),
        cost_estimate=pl.CostEstimate(flops=2 * 10**9, bytes_accessed=2 * 10**6, transcendentals=0),
        name="scored",
    )(*operands)


def whole_step(genotypes, win_lo, win_hi, annotation, chromosome, chi_square):
    samp_rows, block_cols = genotypes.shape
    reach = block_cols // 2
    samp_count = lax.axis_size("samp")
    snp_count = lax.axis_size("snp")
    total_samples = samp_rows * samp_count
    snp_total = block_cols * snp_count
    share = reach // samp_count
    me_samp = lax.axis_index("samp")
    cats = A // snp_count

    lower, upper, sums = counted(genotypes)
    raw_left = from_left(upper, "snp")
    raw_right = from_right(lower, "snp")
    sums = samp_total(sums)
    mean_dose = sums[0] / total_samples
    variance = sums[1] / total_samples - mean_dose * mean_dose
    inverse = lax.rsqrt(variance + 1e-05)

    def standard_of(raw, mean, inv):
        return ((raw.astype(jnp.float32) - mean) * inv).astype(jnp.bfloat16)

    notes = jnp.stack(
        [annotation.astype(jnp.float32), chromosome.astype(jnp.float32), mean_dose, inverse]
    )
    z0 = standard_of(lower, mean_dose[:reach], inverse[:reach])
    z1 = standard_of(upper, mean_dose[reach:], inverse[reach:])
    z0, z1 = lax.optimization_barrier((z0, z1))
    a_id = lax.broadcasted_iota(jnp.int32, (reach, reach), 0)
    b_id = lax.broadcasted_iota(jnp.int32, (reach, reach), 1)

    def fixed(part):
        return jnp.round(part * (FIXED / total_samples)).astype(jnp.int16)

    def turned(parts):
        return [
            lax.dynamic_index_in_dim(parts, (me_samp + step) % samp_count, 0, keepdims=False)
            for step in range(samp_count)
        ]

    def shares(square):
        return square.reshape(samp_count, share, reach)

    near = jnp.concatenate(
        [
            shares(fixed(gram_of(z0, z0))),
            shares(fixed(gram_of(z1, z1))),
            shares(fixed(jnp.where(b_id <= a_id, gram_of(z0, z1), gram_of(z1, z0)))),
        ],
        1,
    )
    near = turned(near)
    near = [near[0]] + [shifted(near[step], "samp", step) for step in range(1, samp_count)]
    notes_left = from_left(notes[:, reach:], "snp")
    notes_right = from_right(notes[:, :reach], "snp")

    z_left = standard_of(raw_left, notes_left[2], notes_left[3])
    z_right = standard_of(raw_right, notes_right[2], notes_right[3])
    right_part = gram_of(z1, z_right)
    edge = jnp.sum(jnp.where(a_id == b_id, right_part, 0.0), 0)
    edge_rows = jnp.zeros((samp_count, 8, reach), jnp.int16)
    edge_rows = edge_rows.at[:, 0, :share].set(fixed(edge).reshape(samp_count, share))
    far = jnp.concatenate(
        [
            shares(fixed(jnp.where(b_id >= a_id, gram_of(z0, z_left), right_part))),
            edge_rows,
        ],
        1,
    )
    far = turned(far)
    far = [far[0]] + [shifted(far[step], "samp", step) for step in range(1, samp_count)]
    near, far, win_lo, win_hi, chi_square = lax.optimization_barrier(
        (near, far, win_lo, win_hi, chi_square)
    )

    grid_of = lambda vector: vector.reshape(-1, share)
    mine = scored(
        near,
        far,
        (notes_left, notes, notes_right),
        (grid_of(win_lo), grid_of(win_hi), grid_of(chi_square)),
        total_samples,
    )
    mine = mine.reshape(snp_count, cats, 2 * share + 2 * A)
    mine = exchange(mine, "snp")
    sums_part = jnp.sum(mine[:, :, 2 * share :], 0)
    score_part = jnp.moveaxis(mine[:, :, : 2 * share], 0, 1).reshape(cats, -1)
    sums_part = samp_total(sums_part)
    sums_whole = to_all(sums_part, "snp").reshape(A, 2 * A)
    parts = [score_part] + [shifted(score_part, "samp", step) for step in range(1, samp_count)]
    turns = jnp.stack([parts[-turn % samp_count] for turn in range(1, 2 * samp_count)])
    both = lax.dynamic_slice_in_dim(turns, samp_count - 1 - me_samp, samp_count, 0)
    split = both.reshape(samp_count, cats, snp_count, 2, share)
    regrouped = jnp.transpose(split, (1, 2, 3, 0, 4)).reshape(cats, snp_total)
    scale = A / snp_total
    gram = scale * sums_whole[:, :A]
    moments = scale * sums_whole[:, A : A + 2].T
    totals = sums_whole[0, A + 2 : A + 4] / snp_total
    return (regrouped, gram, moments, totals)


def solution(mesh):
    in_specs = (P("samp", "snp"), P("snp"), P("snp"), P("snp"), P("snp"), P("snp"))
    out_specs = (P("snp", None), P(), P(), P())
    return jax.shard_map(whole_step, mesh=mesh, in_specs=in_specs, out_specs=out_specs, check_vma=False)
```

time: 218 us -> 120 us (0.55)
  waiting for transfers between devices: 92.3 us -> 26.9 us
  blocking collectives: 62.4 us -> 28 us
  other arithmetic: 18.8 us -> 5.55 us
  Pallas kernels: 0 us -> 9.18 us
  starting transfers between devices: 27 us -> 35.5 us
  local copies, waits for them, and re-layouts: 6.39 us -> 4.1 us
    all_to_all x3 -> x1, waiting for transfers between devices: 70.1 us -> 7.05 us  [exchange(): return lax.all_to_all(array, axis, 0, 0, tiled=True)]
    all_to_all x2 -> x1, blocking collectives: 52.5 us -> 28 us  [exchange(): return lax.all_to_all(array, axis, 0, 0, tiled=True)]
    ppermute x4 -> x19, starting transfers between devices: 12.8 us -> 29.3 us  [the longest x15 17.3 us: shifted(): lax.ppermute(array, axis, [(i, (i + step) % size) for i in range(size)])]
    all_gather x1 -> x0, blocking collectives: 9.9 us -> none  [body(): scores = lax.all_gather(part_scores, 'samp', axis=1, tiled=True)]
    pallas_call x0 -> x2, Pallas kernels: none -> 9.18 us  [the longest x1 7.09 us: counted(): pl.pallas_call(count_kernel, out_shape=(half, half, jax.ShapeDtypeStruct(...]
    reduce_sum x7 -> x1, other arithmetic: 9.02 us -> 0.1 us  [whole_step(): sums_part = jnp.sum(mine[:, :, 2 * share:], 0)]
    all_to_all x3 -> x1, starting transfers between devices: 14.3 us -> 6.18 us  [exchange(): return lax.all_to_all(array, axis, 0, 0, tiled=True)]
    concatenate x3 -> x1, other arithmetic: 3.01 us -> 0.1 us  [whole_step(): jnp.concatenate([shares(fixed(gram_of(z0, z0))), shares(fixed(gram_of(z1,...]
  transfers between devices with their start and end apart: 7 -> 20, of which waited for: 4 -> 8; matrix products, arithmetic and copies ran while one was open for 3% -> 14% of each run, Pallas kernels for 0% -> 0%
where the time goes in v1:
time: 120 us
  starting transfers between devices  35.5 us (30%)
  blocking collectives  28 us (23%)
  waiting for transfers between devices  26.9 us (22%)
  matrix products  9.49 us (8%)
  Pallas kernels  9.18 us (8%)
  other arithmetic  5.55 us (5%)
  local copies, waits for them, and re-layouts  4.1 us (3%)
    all_to_all x1, blocking collectives, exchange(): return lax.all_to_all(array, axis, 0, 0, tiled=True)  28 us
    ppermute x15, starting transfers between devices, shifted(): lax.ppermute(array, axis, [(i, (i + step) % size) for i in range(size)])  17.3 us
    ppermute x15, waiting for transfers between devices, shifted(): lax.ppermute(array, axis, [(i, (i + step) % size) for i in range(size)])  12 us
    dot_general x6, matrix products, gram_of(): lax.dot_general(rows, cols, (((0,), (0,)), ((), ())), preferred_element_t...  9.49 us
    pallas_call x1, Pallas kernels, counted(): pl.pallas_call(count_kernel, out_shape=(half, half, jax.ShapeDtypeStruct(...  7.09 us
    all_to_all x1, waiting for transfers between devices, exchange(): return lax.all_to_all(array, axis, 0, 0, tiled=True)  7.05 us
    ppermute x2, waiting for transfers between devices, from_right(): return lax.ppermute(array, axis, [(i + 1, i) for i in range(count - 1)])  6.99 us
    ppermute x2, starting transfers between devices, from_left(): return lax.ppermute(array, axis, [(i, i + 1) for i in range(count - 1)])  6.66 us
  transfers between devices with their start and end apart: 20, of which 8 were waited for; matrix products, arithmetic and copies ran while one was open for 14% of the time, Pallas kernels for 0%

profile of v1, /device:TPU:1, one launch (start us, length us, event | category | flops | bytes accessed | tf_op | source)
XLA Modules:
  0.0 119.8 jit_solution(2906094596597120721)
XLA Ops:
  0.7 7.1 %counted.1 = (bf16[2048,512]{1,0:T(8,128)(2,1)}, bf16[2048,512]{1,0:T(8,128)(2,1)}, f32[2,1024]{1,0:T(2,128)}) custom-call(s32[2048,1024]{1,0:T(8,128)} %genotypes.1), custom_call_target="tpu_custom_call" | custom-call | tf_op jit(solution)/shard_map/counted/pallas_call | solution.py:83
  7.8 3.8 %collective-permute-start = (f32[2,1024]{1,0:T(2,128)}, f32[2,1024]{1,0:T(2,128)S(1)}, u32[]{:S(2)}, u32[]{:S(2)}) collective-permute-start(f32[2,1024]{1,0:T(2,128)} %get-tuple-element.33), channel_id=1, source_target_pairs={{0,128},{64,192},{128,0},{192,64},{1,129},{65,193},{129,1},{193,65... | collective-permute-start | bytes 24584 | tf_op jit(solution)/shard_map/ppermute | solution.py:25
  12.0 2.3 %collective-permute-start.2 = (f32[2,1024]{1,0:T(2,128)}, f32[2,1024]{1,0:T(2,128)S(1)}, u32[]{:S(2)}, u32[]{:S(2)}) collective-permute-start(f32[2,1024]{1,0:T(2,128)} %get-tuple-element.33), channel_id=1, source_target_pairs={{0,192},{64,0},{128,64},{192,128},{1,193},{65,1},{129,65},{193,129... | collective-permute-start | bytes 24584 | tf_op jit(solution)/shard_map/ppermute | solution.py:25
  14.2 3.4 %collective-permute-start.8 = (bf16[2048,512]{1,0:T(8,128)(2,1)}, bf16[2048,512]{1,0:T(8,128)(2,1)}, u32[]{:S(2)}, u32[]{:S(2)}) collective-permute-start(bf16[2048,512]{1,0:T(8,128)(2,1)} %get-tuple-element.32), channel_id=1, source_target_pairs={{1,0},{2,1},{3,2},{4,3},{5,4},{6,5},{7,6},{8,7},{9,8},{10,9},{11,1... | collective-permute-start | bytes 6291464 | tf_op jit(solution)/shard_map/ppermute | solution.py:40
  17.7 3.0 %collective-permute-start.6 = (bf16[2048,512]{1,0:T(8,128)(2,1)}, bf16[2048,512]{1,0:T(8,128)(2,1)S(1)}, u32[]{:S(2)}, u32[]{:S(2)}) collective-permute-start(bf16[2048,512]{1,0:T(8,128)(2,1)} %get-tuple-element.34), channel_id=1, source_target_pairs={{0,1},{1,2},{2,3},{3,4},{4,5},{5,6},{6,7},{7,8},{8,9},{9,10},{10,1... | collective-permute-start | bytes 6291464 | tf_op jit(solution)/shard_map/ppermute | solution.py:35
  21.6 3.3 %multiply_convert_fusion.2 = (bf16[2048,512]{1,0:T(8,128)(2,1)S(1)}, bf16[2048,512]{1,0:T(8,128)(2,1)S(1)}) fusion(bf16[2048,512]{1,0:T(8,128)(2,1)} %get-tuple-element.34, f32[512]{0:T(512)S(1)} %bitcast.80, f32[512]{0:T(512)S(1)} %bitcast.78, f32[512]{0:T(512)S(1)} %bitcast.81, f32[512]{0:T(512)S(1)} %bitcast.79, bf16[2048,512]{1,0:T(8,128)(2,1)} %get-tuple-element.32), kind=kLoop, calls=%fused_computation.2 | loop fusion | flops 8388608 | bytes 8396800 | tf_op jit(solution)/shard_map/convert_element_type | solution.py:209
  24.9 1.9 %collective-permute-start.9 = (f32[4,512]{1,0:T(4,128)S(1)}, f32[4,512]{1,0:T(4,128)S(1)}, u32[]{:S(2)}, u32[]{:S(2)}) collective-permute-start(f32[4,512]{1,0:T(4,128)S(1)} %get-tuple-element.71), channel_id=1, source_target_pairs={{1,0},{2,1},{3,2},{4,3},{5,4},{6,5},{7,6},{8,7},{9,8},{10,9},{11,1... | collective-permute-start | bytes 24584 | tf_op jit(solution)/shard_map/ppermute | solution.py:40
  26.9 3.6 %collective-permute-start.7 = (f32[4,512]{1,0:T(4,128)S(1)}, f32[4,512]{1,0:T(4,128)S(1)}, u32[]{:S(2)}, u32[]{:S(2)}) collective-permute-start(f32[4,512]{1,0:T(4,128)S(1)} %get-tuple-element.70), channel_id=1, source_target_pairs={{0,1},{1,2},{2,3},{3,4},{4,5},{5,6},{6,7},{7,8},{8,9},{9,10},{10,1... | collective-permute-start | bytes 24584 | tf_op jit(solution)/shard_map/ppermute | solution.py:35
  30.5 1.3 %fusion.15 = s16[512,512]{1,0:T(8,128)(2,1)S(1)} fusion(bf16[2048,512]{1,0:T(8,128)(2,1)S(1)} %get-tuple-element.35), kind=kOutput, calls=%fused_computation.23 | convolution fusion | flops 1074528256 | bytes 2621440 | tf_op jit(solution)/shard_map/dot_general | solution.py:44
  34.4 1.3 %fusion.13 = s16[512,512]{1,0:T(8,128)(2,1)S(1)} fusion(f32[512,512]{1,0:T(8,128)S(1)} %fusion.34, bf16[2048,512]{1,0:T(8,128)(2,1)S(1)} %get-tuple-element.36, bf16[2048,512]{1,0:T(8,128)(2,1)S(1)} %get-tuple-element.35), kind=kOutput, calls=%fused_computation.21 | convolution fusion | flops 1075052544 | bytes 5767168 | tf_op jit(solution)/shard_map/dot_general | solution.py:44
  36.1 7.0 %collective-permute-done.9.refs_10_ = f32[4,512]{1,0:T(4,128)S(1)} collective-permute-done((f32[4,512]{1,0:T(4,128)S(1)}, f32[4,512]{1,0:T(4,128)S(1)}, u32[]{:S(2)}, u32[]{:S(2)}) %collective-permute-start.9) | collective-permute-done | bytes 8224 | tf_op jit(solution)/shard_map/ppermute | solution.py:40
  44.9 2.9 %select_reduce_fusion = (f32[512]{0:T(512)S(1)}, f32[512,512]{1,0:T(8,128)S(1)}) fusion(bf16[2048,512]{1,0:T(8,128)(2,1)S(1)} %get-tuple-element.36, bf16[2048,512]{1,0:T(8,128)(2,1)} %collective-permute-done.8, f32[512]{0:T(512)S(1)} %bitcast.83, f32[512]{0:T(512)S(1)} %bitcast.82), kind=kOutput, calls=%fused_computation.29 | convolution fusion | flops 1078722048 | bytes 5249024 | tf_op jit(solution)/shard_map/dot_general | solution.py:44
  47.9 1.3 %fusion.14 = s16[512,512]{1,0:T(8,128)(2,1)S(1)} fusion(f32[512,512]{1,0:T(8,128)S(1)} %get-tuple-element.83, bf16[2048,512]{1,0:T(8,128)(2,1)S(1)} %get-tuple-element.35, bf16[2048,512]{1,0:T(8,128)(2,1)S(1)} %collective-permute-done.6, f32[512]{0:T(512)S(1)} %bitcast.85, f32[512]{0:T(512)S(1)} %bitcast.84), kind=kOutput, calls=%fused_computation.22 | convolution fusion | flops 1079246848 | bytes 5771264 | tf_op jit(solution)/shard_map/dot_general | solution.py:44
  49.9 2.3 %collective-permute-start.11 = (s16[136,512]{1,0:T(8,128)(2,1)S(1)}, s16[136,512]{1,0:T(8,128)(2,1)S(1)}, u32[]{:S(2)}, u32[]{:S(2)}) collective-permute-start(s16[136,512]{1,0:T(8,128)(2,1)S(1)} %get-tuple-element.67), channel_id=1, source_target_pairs={{0,128},{64,192},{128,0},{192,64},{1,129},{65,193},{129,1},{193,65... | collective-permute-start | bytes 417800 | tf_op jit(solution)/shard_map/ppermute | solution.py:25
  52.3 5.4 %collective-permute-done.3.refs_1_ = s16[384,512]{1,0:T(8,128)(2,1)S(1)} collective-permute-done((s16[384,512]{1,0:T(8,128)(2,1)S(1)}, s16[384,512]{1,0:T(8,128)(2,1)S(1)}, u32[]{:S(2)}, u32[]{:S(2)}) %collective-permute-start.3) | collective-permute-done | bytes 393248 | tf_op jit(solution)/shard_map/ppermute | solution.py:25
  57.7 1.6 %collective-permute-done.5.refs_3_ = s16[384,512]{1,0:T(8,128)(2,1)S(1)} collective-permute-done((s16[384,512]{1,0:T(8,128)(2,1)S(1)}, s16[384,512]{1,0:T(8,128)(2,1)S(1)}, u32[]{:S(2)}, u32[]{:S(2)}) %collective-permute-start.5) | collective-permute-done | bytes 393248 | tf_op jit(solution)/shard_map/ppermute | solution.py:25
  59.3 2.5 %collective-permute-done.10.refs_5_ = s16[136,512]{1,0:T(8,128)(2,1)S(1)} collective-permute-done((s16[136,512]{1,0:T(8,128)(2,1)S(1)}, s16[136,512]{1,0:T(8,128)(2,1)S(1)}, u32[]{:S(2)}, u32[]{:S(2)}) %collective-permute-start.10) | collective-permute-done | bytes 139296 | tf_op jit(solution)/shard_map/ppermute | solution.py:25
  62.7 2.1 %scored.1 = f32[128,512]{1,0:T(8,128)S(1)} custom-call(s16[384,512]{1,0:T(8,128)(2,1)S(1)} %get-tuple-element.37.refs_0_, s16[384,512]{1,0:T(8,128)(2,1)S(1)} %collective-permute-done.3.refs_1_, s16[384,512]{1,0:T(8,128)(2,1)S(1)} %collective-permute-done.4.refs_2_, s16[384,512]{1,0:T(8,128)(2,1)S(1)} %collective-permute-done.5.refs_3_, ...), custom_call_target="tpu_custom_call" | custom-call | flops 2000000000 | bytes 2000000 | tf_op jit(solution)/shard_map/scored/pallas_call | solution.py:178
  64.9 28.0 %all_to_all.10 = f32[64,2,512]{2,1,0:T(2,128)S(1)} all-to-all(f32[64,2,512]{2,1,0:T(2,128)S(1)} %reshape.127), channel_id=1, replica_groups=mesh['samp'=4,'snp'=64] {'snp'}, dimensions={0} | all-to-all | bytes 524288 | tf_op jit(solution)/shard_map/all_to_all | solution.py:15
  93.0 2.5 %collective-permute-start.16 = (f32[2,256]{1,0:T(2,128)S(1)}, f32[2,256]{1,0:T(2,128)S(1)}, u32[]{:S(2)}, u32[]{:S(2)}) collective-permute-start(f32[2,256]{1,0:T(2,128)S(1)} %get-tuple-element.68), channel_id=1, source_target_pairs={{0,128},{64,192},{128,0},{192,64},{1,129},{65,193},{129,1},{193,65... | collective-permute-start | bytes 6152 | tf_op jit(solution)/shard_map/ppermute | solution.py:25
  96.5 1.7 %collective-permute-start.18 = (f32[2,256]{1,0:T(2,128)S(1)}, f32[2,256]{1,0:T(2,128)S(1)}, u32[]{:S(2)}, u32[]{:S(2)}) collective-permute-start(f32[2,256]{1,0:T(2,128)S(1)} %get-tuple-element.68), channel_id=1, source_target_pairs={{0,192},{64,0},{128,64},{192,128},{1,193},{65,1},{129,65},{193,129... | collective-permute-start | bytes 6152 | tf_op jit(solution)/shard_map/ppermute | solution.py:25
  100.6 6.2 %all-to-all-start.1 = ((f32[64,2,256]{2,1,0:T(2,128)}), f32[64,2,256]{2,1,0:T(2,128)S(1)}, u32[]{:S(2)}, u32[]{:S(2)}) async-start(f32[64,2,256]{2,1,0:T(2,128)} %broadcast_in_dim.7), calls=%async_computation.1 | async-start | bytes 262144 | tf_op jit(solution)/shard_map/all_to_all | solution.py:15
  106.8 1.6 %collective-permute-done.15 = f32[2,16384]{1,0:T(2,128)S(1)} collective-permute-done((f32[2,16384]{1,0:T(2,128)S(1)}, f32[2,16384]{1,0:T(2,128)S(1)}, u32[]{:S(2)}, u32[]{:S(2)}) %collective-permute-start.15) | collective-permute-done | bytes 131104 | tf_op jit(solution)/shard_map/ppermute | solution.py:25
  110.8 7.0 %all-to-all-done.1 = f32[64,2,256]{2,1,0:T(2,128)S(1)} async-done(((f32[64,2,256]{2,1,0:T(2,128)}), f32[64,2,256]{2,1,0:T(2,128)S(1)}, u32[]{:S(2)}, u32[]{:S(2)}) %all-to-all-start.1) | async-done | bytes 131104 | tf_op jit(solution)/shard_map/all_to_all | solution.py:15
  (71 shorter events, 15.4 us)
Async XLA Ops:
  0.6 20.1 %copy-start.3 = (s32[1024]{0:T(1024)S(1)}, s32[1024]{0:T(1024)}, u32[]{:S(2)}) copy-start(s32[1024]{0:T(1024)} %param.11) | copy-start | bytes 12292
  0.6 20.1 %copy-start.4 = (s32[1024]{0:T(1024)S(1)}, s32[1024]{0:T(1024)}, u32[]{:S(2)}) copy-start(s32[1024]{0:T(1024)} %param.12) | copy-start | bytes 12292
  7.8 13.1 %collective-permute-start = (f32[2,1024]{1,0:T(2,128)}, f32[2,1024]{1,0:T(2,128)S(1)}, u32[]{:S(2)}, u32[]{:S(2)}) collective-permute-start(f32[2,1024]{1,0:T(2,128)} %get-tuple-element.33), channel_id=1, source_target_pairs={{0,128},{64,192},{128,0},{192,64},{1,129},{65,193},{129,1},{193,65... | collective-permute-start | bytes 24584 | tf_op jit(solution)/shard_map/ppermute | solution.py:25
  11.6 9.3 %collective-permute-start.1 = (f32[2,1024]{1,0:T(2,128)}, f32[2,1024]{1,0:T(2,128)S(1)}, u32[]{:S(2)}, u32[]{:S(2)}) collective-permute-start(f32[2,1024]{1,0:T(2,128)} %get-tuple-element.33), channel_id=1, source_target_pairs={{0,64},{64,128},{128,192},{192,0},{1,65},{65,129},{129,193},{193,1... | collective-permute-start | bytes 24584 | tf_op jit(solution)/shard_map/ppermute | solution.py:25
  12.0 8.9 %collective-permute-start.2 = (f32[2,1024]{1,0:T(2,128)}, f32[2,1024]{1,0:T(2,128)S(1)}, u32[]{:S(2)}, u32[]{:S(2)}) collective-permute-start(f32[2,1024]{1,0:T(2,128)} %get-tuple-element.33), channel_id=1, source_target_pairs={{0,192},{64,0},{128,64},{192,128},{1,193},{65,1},{129,65},{193,129... | collective-permute-start | bytes 24584 | tf_op jit(solution)/shard_map/ppermute | solution.py:25
  14.2 30.7 %collective-permute-start.8 = (bf16[2048,512]{1,0:T(8,128)(2,1)}, bf16[2048,512]{1,0:T(8,128)(2,1)}, u32[]{:S(2)}, u32[]{:S(2)}) collective-permute-start(bf16[2048,512]{1,0:T(8,128)(2,1)} %get-tuple-element.32), channel_id=1, source_target_pairs={{1,0},{2,1},{3,2},{4,3},{5,4},{6,5},{7,6},{8,7},{9,8},{10,9},{11,1... | collective-permute-start | bytes 6291464 | tf_op jit(solution)/shard_map/ppermute | solution.py:40
  17.7 30.2 %collective-permute-start.6 = (bf16[2048,512]{1,0:T(8,128)(2,1)}, bf16[2048,512]{1,0:T(8,128)(2,1)S(1)}, u32[]{:S(2)}, u32[]{:S(2)}) collective-permute-start(bf16[2048,512]{1,0:T(8,128)(2,1)} %get-tuple-element.34), channel_id=1, source_target_pairs={{0,1},{1,2},{2,3},{3,4},{4,5},{5,6},{6,7},{7,8},{8,9},{9,10},{10,1... | collective-permute-start | bytes 6291464 | tf_op jit(solution)/shard_map/ppermute | solution.py:35
  24.9 18.1 %collective-permute-start.9 = (f32[4,512]{1,0:T(4,128)S(1)}, f32[4,512]{1,0:T(4,128)S(1)}, u32[]{:S(2)}, u32[]{:S(2)}) collective-permute-start(f32[4,512]{1,0:T(4,128)S(1)} %get-tuple-element.71), channel_id=1, source_target_pairs={{1,0},{2,1},{3,2},{4,3},{5,4},{6,5},{7,6},{8,7},{9,8},{10,9},{11,1... | collective-permute-start | bytes 24584 | tf_op jit(solution)/shard_map/ppermute | solution.py:40
  26.9 17.1 %collective-permute-start.7 = (f32[4,512]{1,0:T(4,128)S(1)}, f32[4,512]{1,0:T(4,128)S(1)}, u32[]{:S(2)}, u32[]{:S(2)}) collective-permute-start(f32[4,512]{1,0:T(4,128)S(1)} %get-tuple-element.70), channel_id=1, source_target_pairs={{0,1},{1,2},{2,3},{3,4},{4,5},{5,6},{6,7},{7,8},{8,9},{9,10},{10,1... | collective-permute-start | bytes 24584 | tf_op jit(solution)/shard_map/ppermute | solution.py:35
  36.0 21.7 %collective-permute-start.3 = (s16[384,512]{1,0:T(8,128)(2,1)S(1)}, s16[384,512]{1,0:T(8,128)(2,1)S(1)}, u32[]{:S(2)}, u32[]{:S(2)}) collective-permute-start(s16[384,512]{1,0:T(8,128)(2,1)S(1)} %get-tuple-element.62), channel_id=1, source_target_pairs={{0,64},{64,128},{128,192},{192,0},{1,65},{65,129},{129,193},{193,1... | collective-permute-start | bytes 1179656 | tf_op jit(solution)/shard_map/ppermute | solution.py:25
  43.1 14.7 %collective-permute-start.4 = (s16[384,512]{1,0:T(8,128)(2,1)S(1)}, s16[384,512]{1,0:T(8,128)(2,1)S(1)}, u32[]{:S(2)}, u32[]{:S(2)}) collective-permute-start(s16[384,512]{1,0:T(8,128)(2,1)S(1)} %get-tuple-element.61), channel_id=1, source_target_pairs={{0,128},{64,192},{128,0},{192,64},{1,129},{65,193},{129,1},{193,65... | collective-permute-start | bytes 1179656 | tf_op jit(solution)/shard_map/ppermute | solution.py:25
  44.0 15.3 %collective-permute-start.5 = (s16[384,512]{1,0:T(8,128)(2,1)S(1)}, s16[384,512]{1,0:T(8,128)(2,1)S(1)}, u32[]{:S(2)}, u32[]{:S(2)}) collective-permute-start(s16[384,512]{1,0:T(8,128)(2,1)S(1)} %get-tuple-element.60), channel_id=1, source_target_pairs={{0,192},{64,0},{128,64},{192,128},{1,193},{65,1},{129,65},{193,129... | collective-permute-start | bytes 1179656 | tf_op jit(solution)/shard_map/ppermute | solution.py:25
  47.9 14.8 %copy-start = (s32[1024]{0:T(1024)S(1)}, s32[1024]{0:T(1024)}, u32[]{:S(2)}) copy-start(s32[1024]{0:T(1024)} %param.9) | copy-start | bytes 12292
  47.9 14.8 %copy-start.1 = (s32[1024]{0:T(1024)S(1)}, s32[1024]{0:T(1024)}, u32[]{:S(2)}) copy-start(s32[1024]{0:T(1024)} %param.10) | copy-start | bytes 12292
  49.3 12.4 %collective-permute-start.10 = (s16[136,512]{1,0:T(8,128)(2,1)S(1)}, s16[136,512]{1,0:T(8,128)(2,1)S(1)}, u32[]{:S(2)}, u32[]{:S(2)}) collective-permute-start(s16[136,512]{1,0:T(8,128)(2,1)S(1)} %get-tuple-element.66), channel_id=1, source_target_pairs={{0,64},{64,128},{128,192},{192,0},{1,65},{65,129},{129,193},{193,1... | collective-permute-start | bytes 417800 | tf_op jit(solution)/shard_map/ppermute | solution.py:25
  49.9 11.8 %collective-permute-start.11 = (s16[136,512]{1,0:T(8,128)(2,1)S(1)}, s16[136,512]{1,0:T(8,128)(2,1)S(1)}, u32[]{:S(2)}, u32[]{:S(2)}) collective-permute-start(s16[136,512]{1,0:T(8,128)(2,1)S(1)} %get-tuple-element.67), channel_id=1, source_target_pairs={{0,128},{64,192},{128,0},{192,64},{1,129},{65,193},{129,1},{193,65... | collective-permute-start | bytes 417800 | tf_op jit(solution)/shard_map/ppermute | solution.py:25
  57.7 4.9 %collective-permute-start.12 = (s16[136,512]{1,0:T(8,128)(2,1)S(1)}, s16[136,512]{1,0:T(8,128)(2,1)S(1)}, u32[]{:S(2)}, u32[]{:S(2)}) collective-permute-start(s16[136,512]{1,0:T(8,128)(2,1)S(1)} %get-tuple-element.64), channel_id=1, source_target_pairs={{0,192},{64,0},{128,64},{192,128},{1,193},{65,1},{129,65},{193,129... | collective-permute-start | bytes 417800 | tf_op jit(solution)/shard_map/ppermute | solution.py:25
  93.0 6.8 %collective-permute-start.16 = (f32[2,256]{1,0:T(2,128)S(1)}, f32[2,256]{1,0:T(2,128)S(1)}, u32[]{:S(2)}, u32[]{:S(2)}) collective-permute-start(f32[2,256]{1,0:T(2,128)S(1)} %get-tuple-element.68), channel_id=1, source_target_pairs={{0,128},{64,192},{128,0},{192,64},{1,129},{65,193},{129,1},{193,65... | collective-permute-start | bytes 6152 | tf_op jit(solution)/shard_map/ppermute | solution.py:25
  95.5 4.3 %collective-permute-start.17 = (f32[2,256]{1,0:T(2,128)S(1)}, f32[2,256]{1,0:T(2,128)S(1)}, u32[]{:S(2)}, u32[]{:S(2)}) collective-permute-start(f32[2,256]{1,0:T(2,128)S(1)} %get-tuple-element.68), channel_id=1, source_target_pairs={{0,64},{64,128},{128,192},{192,0},{1,65},{65,129},{129,193},{193,1... | collective-permute-start | bytes 6152 | tf_op jit(solution)/shard_map/ppermute | solution.py:25
  96.5 3.4 %collective-permute-start.18 = (f32[2,256]{1,0:T(2,128)S(1)}, f32[2,256]{1,0:T(2,128)S(1)}, u32[]{:S(2)}, u32[]{:S(2)}) collective-permute-start(f32[2,256]{1,0:T(2,128)S(1)} %get-tuple-element.68), channel_id=1, source_target_pairs={{0,192},{64,0},{128,64},{192,128},{1,193},{65,1},{129,65},{193,129... | collective-permute-start | bytes 6152 | tf_op jit(solution)/shard_map/ppermute | solution.py:25
  98.2 8.6 %collective-permute-start.13 = (f32[2,16384]{1,0:T(2,128)S(1)}, f32[2,16384]{1,0:T(2,128)S(1)}, u32[]{:S(2)}, u32[]{:S(2)}) collective-permute-start(f32[2,16384]{1,0:T(2,128)S(1)} %bitcast.69), channel_id=1, source_target_pairs={{0,192},{64,0},{128,64},{192,128},{1,193},{65,1},{129,65},{193,129... | collective-permute-start | bytes 393224 | tf_op jit(solution)/shard_map/ppermute | solution.py:25
  99.3 7.5 %collective-permute-start.14 = (f32[2,16384]{1,0:T(2,128)S(1)}, f32[2,16384]{1,0:T(2,128)S(1)}, u32[]{:S(2)}, u32[]{:S(2)}) collective-permute-start(f32[2,16384]{1,0:T(2,128)S(1)} %bitcast.70), channel_id=1, source_target_pairs={{0,128},{64,192},{128,0},{192,64},{1,129},{65,193},{129,1},{193,65... | collective-permute-start | bytes 393224 | tf_op jit(solution)/shard_map/ppermute | solution.py:25
  99.8 8.6 %collective-permute-start.15 = (f32[2,16384]{1,0:T(2,128)S(1)}, f32[2,16384]{1,0:T(2,128)S(1)}, u32[]{:S(2)}, u32[]{:S(2)}) collective-permute-start(f32[2,16384]{1,0:T(2,128)S(1)} %bitcast.71), channel_id=1, source_target_pairs={{0,64},{64,128},{128,192},{192,0},{1,65},{65,129},{129,193},{193,1... | collective-permute-start | bytes 393224 | tf_op jit(solution)/shard_map/ppermute | solution.py:25
  100.6 17.3 %all-to-all-start.1 = ((f32[64,2,256]{2,1,0:T(2,128)}), f32[64,2,256]{2,1,0:T(2,128)S(1)}, u32[]{:S(2)}, u32[]{:S(2)}) async-start(f32[64,2,256]{2,1,0:T(2,128)} %broadcast_in_dim.7), calls=%async_computation.1 | async-start | bytes 262144 | tf_op jit(solution)/shard_map/all_to_all | solution.py:15
  (1 other events, 14.8 us)

commit v2 on v1

--- a/solution.py
+++ b/solution.py
@@ -79,14 +79,14 @@
 def counted(genotypes):
     rows, cols = genotypes.shape
     step = rows // 16
-    half = jax.ShapeDtypeStruct((rows, cols // 2), jnp.bfloat16)
+    half = pltpu.VMEM((rows, cols // 2), jnp.bfloat16)
     return pl.pallas_call(
         count_kernel,
         out_shape=(half, half, jax.ShapeDtypeStruct((2, cols), jnp.float32)),
         in_specs=[pl.BlockSpec(memory_space=pl.ANY)],
         out_specs=(pl.BlockSpec(memory_space=pltpu.VMEM),) * 3,
         scratch_shapes=[pltpu.VMEM((4, step, cols), jnp.int32), pltpu.SemaphoreType.DMA((4,))],
-        compiler_params=pltpu.CompilerParams(vmem_limit_bytes=57 * 2**20),
+        compiler_params=pltpu.CompilerParams(vmem_limit_bytes=54 * 2**20),
         name="counted",
     )(genotypes)
 
@@ -186,6 +186,24 @@
     )(*operands)
 
 
+def last_kernel(scale, count, whole, gram, moments, totals):
+    gram[...] = scale * whole[:, :A]
+    moments[...] = scale * jnp.transpose(whole[:, A:])[0:2, :]
+    totals[...] = whole[0:1, A + 2 : A + 4] / count
+
+
+def finished(whole, scale, count):
+    shapes = ((A, A), (2, A), (1, 2))
+    return pl.pallas_call(
+        functools.partial(last_kernel, scale, count),
+        out_shape=tuple(jax.ShapeDtypeStruct(shape, jnp.float32) for shape in shapes),
+        in_specs=[pl.BlockSpec(memory_space=pltpu.VMEM)],
+        out_specs=(pl.BlockSpec(memory_space=pltpu.VMEM),) * 3,
+        compiler_params=pltpu.CompilerParams(vmem_limit_bytes=4 * 2**20),
+        name="finished",
+    )(whole)
+
+
 def whole_step(genotypes, win_lo, win_hi, annotation, chromosome, chi_square):
     samp_rows, block_cols = genotypes.shape
     reach = block_cols // 2
@@ -198,8 +216,8 @@
     cats = A // snp_count
 
     lower, upper, sums = counted(genotypes)
+    raw_right = from_right(lower, "snp")
     raw_left = from_left(upper, "snp")
-    raw_right = from_right(lower, "snp")
     sums = samp_total(sums)
     mean_dose = sums[0] / total_samples
     variance = sums[1] / total_samples - mean_dose * mean_dose
@@ -239,13 +257,16 @@
     )
     near = turned(near)
     near = [near[0]] + [shifted(near[step], "samp", step) for step in range(1, samp_count)]
+    notes_right = from_right(notes[:, :reach], "snp")
     notes_left = from_left(notes[:, reach:], "snp")
-    notes_right = from_right(notes[:, :reach], "snp")
-
-    z_left = standard_of(raw_left, notes_left[2], notes_left[3])
+
     z_right = standard_of(raw_right, notes_right[2], notes_right[3])
     right_part = gram_of(z1, z_right)
     edge = jnp.sum(jnp.where(a_id == b_id, right_part, 0.0), 0)
+    right_part, edge, raw_left, notes_left = lax.optimization_barrier(
+        (right_part, edge, raw_left, notes_left)
+    )
+    z_left = standard_of(raw_left, notes_left[2], notes_left[3])
     edge_rows = jnp.zeros((samp_count, 8, reach), jnp.int16)
     edge_rows = edge_rows.at[:, 0, :share].set(fixed(edge).reshape(samp_count, share))
     far = jnp.concatenate(
@@ -280,11 +301,8 @@
     both = lax.dynamic_slice_in_dim(turns, samp_count - 1 - me_samp, samp_count, 0)
     split = both.reshape(samp_count, cats, snp_count, 2, share)
     regrouped = jnp.transpose(split, (1, 2, 3, 0, 4)).reshape(cats, snp_total)
-    scale = A / snp_total
-    gram = scale * sums_whole[:, :A]
-    moments = scale * sums_whole[:, A : A + 2].T
-    totals = sums_whole[0, A + 2 : A + 4] / snp_total
-    return (regrouped, gram, moments, totals)
+    gram, moments, totals = finished(sums_whole, A / snp_total, snp_total)
+    return (regrouped, gram, moments, totals.reshape(2))
 
 
 def solution(mesh):

time: 120 us -> 119 us (level)
  other arithmetic: 5.55 us -> 3.69 us
  waiting for transfers between devices: 26.9 us -> 25.1 us
  matrix products: 9.49 us -> 11.1 us
    dot_general x6, matrix products: 9.49 us -> 11.1 us  [gram_of(): lax.dot_general(rows, cols, (((0,), (0,)), ((), ())), preferred_element_t...]
    ppermute x15, waiting for transfers between devices: 12 us -> 10.4 us  [shifted(): lax.ppermute(array, axis, [(i, (i + step) % size) for i in range(size)])]
  transfers between devices with their start and end apart: 20 -> 20, of which waited for: 8 -> 7; matrix products, arithmetic and copies ran while one was open for 14% -> 15% of each run, Pallas kernels for 0% -> 0%
where the time goes in v2:
time: 119 us; the launch traced here: 118 us
  starting transfers between devices  36.3 us (31%)
  blocking collectives  27.9 us (23%)
  waiting for transfers between devices  25.1 us (21%)
  matrix products  11.1 us (9%)
  Pallas kernels  9.21 us (8%)
  other arithmetic  3.69 us (3%)
  local copies, waits for them, and re-layouts  3.46 us (3%)
    all_to_all x1, blocking collectives, exchange(): return lax.all_to_all(array, axis, 0, 0, tiled=True)  27.9 us
    ppermute x15, starting transfers between devices, shifted(): lax.ppermute(array, axis, [(i, (i + step) % size) for i in range(size)])  18.1 us
    dot_general x6, matrix products, gram_of(): lax.dot_general(rows, cols, (((0,), (0,)), ((), ())), preferred_element_t...  11.1 us
    ppermute x15, waiting for transfers between devices, shifted(): lax.ppermute(array, axis, [(i, (i + step) % size) for i in range(size)])  10.4 us
    ppermute x2, waiting for transfers between devices, from_right(): return lax.ppermute(array, axis, [(i + 1, i) for i in range(count - 1)])  7.62 us
    all_to_all x1, waiting for transfers between devices, exchange(): return lax.all_to_all(array, axis, 0, 0, tiled=True)  7.06 us
    pallas_call x1, Pallas kernels, counted(): pl.pallas_call(count_kernel, out_shape=(half, half, jax.ShapeDtypeStruct(...  6.47 us
    all_to_all x1, starting transfers between devices, exchange(): return lax.all_to_all(array, axis, 0, 0, tiled=True)  6.18 us
  transfers between devices with their start and end apart: 20, of which 7 were waited for; matrix products, arithmetic and copies ran while one was open for 15% of the time, Pallas kernels for 0%

profile of v2, /device:TPU:1, one launch (start us, length us, event | category | flops | bytes accessed | tf_op | source)
XLA Modules:
  0.0 117.9 jit_solution(1038513801237992042)
XLA Ops:
  0.7 6.5 %counted.1 = (bf16[2048,512]{1,0:T(8,128)(2,1)}, bf16[2048,512]{1,0:T(8,128)(2,1)S(1)}, f32[2,1024]{1,0:T(2,128)}) custom-call(s32[2048,1024]{1,0:T(8,128)} %genotypes.1), custom_call_target="tpu_custom_call" | custom-call | tf_op jit(solution)/shard_map/counted/pallas_call | solution.py:83
  7.1 3.8 %collective-permute-start = (f32[2,1024]{1,0:T(2,128)}, f32[2,1024]{1,0:T(2,128)S(1)}, u32[]{:S(2)}, u32[]{:S(2)}) collective-permute-start(f32[2,1024]{1,0:T(2,128)} %get-tuple-element.40), channel_id=1, source_target_pairs={{0,128},{64,192},{128,0},{192,64},{1,129},{65,193},{129,1},{193,65... | collective-permute-start | bytes 24584 | tf_op jit(solution)/shard_map/ppermute | solution.py:25
  11.3 2.3 %collective-permute-start.2 = (f32[2,1024]{1,0:T(2,128)}, f32[2,1024]{1,0:T(2,128)S(1)}, u32[]{:S(2)}, u32[]{:S(2)}) collective-permute-start(f32[2,1024]{1,0:T(2,128)} %get-tuple-element.40), channel_id=1, source_target_pairs={{0,192},{64,0},{128,64},{192,128},{1,193},{65,1},{129,65},{193,129... | collective-permute-start | bytes 24584 | tf_op jit(solution)/shard_map/ppermute | solution.py:25
  13.6 3.4 %collective-permute-start.6 = (bf16[2048,512]{1,0:T(8,128)(2,1)}, bf16[2048,512]{1,0:T(8,128)(2,1)}, u32[]{:S(2)}, u32[]{:S(2)}) collective-permute-start(bf16[2048,512]{1,0:T(8,128)(2,1)} %get-tuple-element.39), channel_id=1, source_target_pairs={{1,0},{2,1},{3,2},{4,3},{5,4},{6,5},{7,6},{8,7},{9,8},{10,9},{11,1... | collective-permute-start | bytes 6291464 | tf_op jit(solution)/shard_map/ppermute | solution.py:40
  17.0 3.0 %collective-permute-start.8 = (bf16[2048,512]{1,0:T(8,128)(2,1)S(1)}, bf16[2048,512]{1,0:T(8,128)(2,1)}, u32[]{:S(2)}, u32[]{:S(2)}) collective-permute-start(bf16[2048,512]{1,0:T(8,128)(2,1)S(1)} %get-tuple-element.41), channel_id=1, source_target_pairs={{0,1},{1,2},{2,3},{3,4},{4,5},{5,6},{6,7},{7,8},{8,9},{9,10},{10,1... | collective-permute-start | bytes 6291464 | tf_op jit(solution)/shard_map/ppermute | solution.py:35
  21.0 2.7 %multiply_convert_fusion.2 = (bf16[2048,512]{1,0:T(8,128)(2,1)S(1)}, bf16[2048,512]{1,0:T(8,128)(2,1)S(1)}) fusion(bf16[2048,512]{1,0:T(8,128)(2,1)S(1)} %get-tuple-element.41, f32[512]{0:T(512)S(1)} %bitcast.77, f32[512]{0:T(512)S(1)} %bitcast.75, f32[512]{0:T(512)S(1)} %bitcast.78, f32[512]{0:T(512)S(1)} %bitcast.76, bf16[2048,512]{1,0:T(8,128)(2,1)} %get-tuple-element.39), kind=kLoop, calls=%fused_computation.2 | loop fusion | flops 8388608 | bytes 8396800 | tf_op jit(solution)/shard_map/convert_element_type | solution.py:227
  23.7 2.6 %collective-permute-start.7 = (f32[4,512]{1,0:T(4,128)S(1)}, f32[4,512]{1,0:T(4,128)S(1)}, u32[]{:S(2)}, u32[]{:S(2)}) collective-permute-start(f32[4,512]{1,0:T(4,128)S(1)} %get-tuple-element.73), channel_id=1, source_target_pairs={{1,0},{2,1},{3,2},{4,3},{5,4},{6,5},{7,6},{8,7},{9,8},{10,9},{11,1... | collective-permute-start | bytes 24584 | tf_op jit(solution)/shard_map/ppermute | solution.py:40
  26.3 3.0 %collective-permute-start.9 = (f32[4,512]{1,0:T(4,128)S(1)}, f32[4,512]{1,0:T(4,128)S(1)}, u32[]{:S(2)}, u32[]{:S(2)}) collective-permute-start(f32[4,512]{1,0:T(4,128)S(1)} %get-tuple-element.72), channel_id=1, source_target_pairs={{0,1},{1,2},{2,3},{3,4},{4,5},{5,6},{6,7},{7,8},{8,9},{9,10},{10,1... | collective-permute-start | bytes 24584 | tf_op jit(solution)/shard_map/ppermute | solution.py:35
  33.2 1.3 %fusion.13 = s16[512,512]{1,0:T(8,128)(2,1)S(1)} fusion(f32[512,512]{1,0:T(8,128)S(1)} %fusion.32, bf16[2048,512]{1,0:T(8,128)(2,1)S(1)} %get-tuple-element.43, bf16[2048,512]{1,0:T(8,128)(2,1)S(1)} %get-tuple-element.42), kind=kOutput, calls=%fused_computation.21 | convolution fusion | flops 1075052544 | bytes 5767168 | tf_op jit(solution)/shard_map/dot_general | solution.py:44
  34.8 7.6 %collective-permute-done.7.refs_10_ = f32[4,512]{1,0:T(4,128)S(1)} collective-permute-done((f32[4,512]{1,0:T(4,128)S(1)}, f32[4,512]{1,0:T(4,128)S(1)}, u32[]{:S(2)}, u32[]{:S(2)}) %collective-permute-start.7) | collective-permute-done | bytes 8224 | tf_op jit(solution)/shard_map/ppermute | solution.py:40
  42.5 1.8 %collective-permute-start.5 = (s16[384,512]{1,0:T(8,128)(2,1)S(1)}, s16[384,512]{1,0:T(8,128)(2,1)S(1)}, u32[]{:S(2)}, u32[]{:S(2)}) collective-permute-start(s16[384,512]{1,0:T(8,128)(2,1)S(1)} %get-tuple-element.62), channel_id=1, source_target_pairs={{0,192},{64,0},{128,64},{192,128},{1,193},{65,1},{129,65},{193,129... | collective-permute-start | bytes 1179656 | tf_op jit(solution)/shard_map/ppermute | solution.py:25
  44.3 2.9 %select_reduce_fusion = (f32[512]{0:T(512)S(1)}, f32[512,512]{1,0:T(8,128)S(1)}) fusion(bf16[2048,512]{1,0:T(8,128)(2,1)S(1)} %get-tuple-element.43, bf16[2048,512]{1,0:T(8,128)(2,1)} %collective-permute-done.6, f32[512]{0:T(512)S(1)} %bitcast.80, f32[512]{0:T(512)S(1)} %bitcast.79), kind=kOutput, calls=%fused_computation.29 | convolution fusion | flops 1078722048 | bytes 5249024 | tf_op jit(solution)/shard_map/dot_general | solution.py:44
  47.3 3.0 %fusion.14 = s16[512,512]{1,0:T(8,128)(2,1)S(1)} fusion(f32[512,512]{1,0:T(8,128)S(1)} %get-tuple-element.46, bf16[2048,512]{1,0:T(8,128)(2,1)S(1)} %get-tuple-element.42, bf16[2048,512]{1,0:T(8,128)(2,1)} %collective-permute-done.8, f32[512]{0:T(512)S(1)} %bitcast.82, f32[512]{0:T(512)S(1)} %bitcast.81), kind=kOutput, calls=%fused_computation.22 | convolution fusion | flops 1079246848 | bytes 5771264 | tf_op jit(solution)/shard_map/dot_general | solution.py:44
  50.4 2.8 %collective-permute-start.11 = (s16[136,512]{1,0:T(8,128)(2,1)S(1)}, s16[136,512]{1,0:T(8,128)(2,1)S(1)}, u32[]{:S(2)}, u32[]{:S(2)}) collective-permute-start(s16[136,512]{1,0:T(8,128)(2,1)S(1)} %get-tuple-element.69), channel_id=1, source_target_pairs={{0,128},{64,192},{128,0},{192,64},{1,129},{65,193},{129,1},{193,65... | collective-permute-start | bytes 417800 | tf_op jit(solution)/shard_map/ppermute | solution.py:25
  53.3 2.4 %collective-permute-done.3.refs_1_ = s16[384,512]{1,0:T(8,128)(2,1)S(1)} collective-permute-done((s16[384,512]{1,0:T(8,128)(2,1)S(1)}, s16[384,512]{1,0:T(8,128)(2,1)S(1)}, u32[]{:S(2)}, u32[]{:S(2)}) %collective-permute-start.3) | collective-permute-done | bytes 393248 | tf_op jit(solution)/shard_map/ppermute | solution.py:25
  55.7 2.2 %collective-permute-done.5.refs_3_ = s16[384,512]{1,0:T(8,128)(2,1)S(1)} collective-permute-done((s16[384,512]{1,0:T(8,128)(2,1)S(1)}, s16[384,512]{1,0:T(8,128)(2,1)S(1)}, u32[]{:S(2)}, u32[]{:S(2)}) %collective-permute-start.5) | collective-permute-done | bytes 393248 | tf_op jit(solution)/shard_map/ppermute | solution.py:25
  57.9 3.5 %collective-permute-done.10.refs_5_ = s16[136,512]{1,0:T(8,128)(2,1)S(1)} collective-permute-done((s16[136,512]{1,0:T(8,128)(2,1)S(1)}, s16[136,512]{1,0:T(8,128)(2,1)S(1)}, u32[]{:S(2)}, u32[]{:S(2)}) %collective-permute-start.10) | collective-permute-done | bytes 139296 | tf_op jit(solution)/shard_map/ppermute | solution.py:25
  62.1 2.1 %scored.1 = f32[128,512]{1,0:T(8,128)S(1)} custom-call(s16[384,512]{1,0:T(8,128)(2,1)S(1)} %get-tuple-element.48.refs_0_, s16[384,512]{1,0:T(8,128)(2,1)S(1)} %collective-permute-done.3.refs_1_, s16[384,512]{1,0:T(8,128)(2,1)S(1)} %collective-permute-done.4.refs_2_, s16[384,512]{1,0:T(8,128)(2,1)S(1)} %collective-permute-done.5.refs_3_, ...), custom_call_target="tpu_custom_call" | custom-call | flops 2000000000 | bytes 2000000 | tf_op jit(solution)/shard_map/scored/pallas_call | solution.py:178
  64.4 27.9 %all_to_all.10 = f32[64,2,512]{2,1,0:T(2,128)S(1)} all-to-all(f32[64,2,512]{2,1,0:T(2,128)S(1)} %reshape.111), channel_id=1, replica_groups=mesh['samp'=4,'snp'=64] {'snp'}, dimensions={0} | all-to-all | bytes 524288 | tf_op jit(solution)/shard_map/all_to_all | solution.py:15
  92.4 2.5 %collective-permute-start.16 = (f32[2,256]{1,0:T(2,128)S(1)}, f32[2,256]{1,0:T(2,128)S(1)}, u32[]{:S(2)}, u32[]{:S(2)}) collective-permute-start(f32[2,256]{1,0:T(2,128)S(1)} %get-tuple-element.70), channel_id=1, source_target_pairs={{0,128},{64,192},{128,0},{192,64},{1,129},{65,193},{129,1},{193,65... | collective-permute-start | bytes 6152 | tf_op jit(solution)/shard_map/ppermute | solution.py:25
  95.8 1.7 %collective-permute-start.18 = (f32[2,256]{1,0:T(2,128)S(1)}, f32[2,256]{1,0:T(2,128)S(1)}, u32[]{:S(2)}, u32[]{:S(2)}) collective-permute-start(f32[2,256]{1,0:T(2,128)S(1)} %get-tuple-element.70), channel_id=1, source_target_pairs={{0,192},{64,0},{128,64},{192,128},{1,193},{65,1},{129,65},{193,129... | collective-permute-start | bytes 6152 | tf_op jit(solution)/shard_map/ppermute | solution.py:25
  99.9 6.2 %all-to-all-start.1 = ((f32[64,2,256]{2,1,0:T(2,128)}), f32[64,2,256]{2,1,0:T(2,128)S(1)}, u32[]{:S(2)}, u32[]{:S(2)}) async-start(f32[64,2,256]{2,1,0:T(2,128)} %broadcast_in_dim.7), calls=%async_computation.1 | async-start | bytes 262144 | tf_op jit(solution)/shard_map/all_to_all | solution.py:15
  106.1 1.6 %collective-permute-done.15 = f32[2,16384]{1,0:T(2,128)S(1)} collective-permute-done((f32[2,16384]{1,0:T(2,128)S(1)}, f32[2,16384]{1,0:T(2,128)S(1)}, u32[]{:S(2)}, u32[]{:S(2)}) %collective-permute-start.15) | collective-permute-done | bytes 131104 | tf_op jit(solution)/shard_map/ppermute | solution.py:25
  110.1 7.1 %all-to-all-done.1 = f32[64,2,256]{2,1,0:T(2,128)S(1)} async-done(((f32[64,2,256]{2,1,0:T(2,128)}), f32[64,2,256]{2,1,0:T(2,128)S(1)}, u32[]{:S(2)}, u32[]{:S(2)}) %all-to-all-start.1) | async-done | bytes 131104 | tf_op jit(solution)/shard_map/all_to_all | solution.py:15
  (68 shorter events, 12.9 us)
Async XLA Ops:
  0.6 19.5 %copy-start.3 = (s32[1024]{0:T(1024)S(1)}, s32[1024]{0:T(1024)}, u32[]{:S(2)}) copy-start(s32[1024]{0:T(1024)} %param.11) | copy-start | bytes 12292
  0.6 19.5 %copy-start.4 = (s32[1024]{0:T(1024)S(1)}, s32[1024]{0:T(1024)}, u32[]{:S(2)}) copy-start(s32[1024]{0:T(1024)} %param.12) | copy-start | bytes 12292
  7.1 13.1 %collective-permute-start = (f32[2,1024]{1,0:T(2,128)}, f32[2,1024]{1,0:T(2,128)S(1)}, u32[]{:S(2)}, u32[]{:S(2)}) collective-permute-start(f32[2,1024]{1,0:T(2,128)} %get-tuple-element.40), channel_id=1, source_target_pairs={{0,128},{64,192},{128,0},{192,64},{1,129},{65,193},{129,1},{193,65... | collective-permute-start | bytes 24584 | tf_op jit(solution)/shard_map/ppermute | solution.py:25
  10.9 9.3 %collective-permute-start.1 = (f32[2,1024]{1,0:T(2,128)}, f32[2,1024]{1,0:T(2,128)S(1)}, u32[]{:S(2)}, u32[]{:S(2)}) collective-permute-start(f32[2,1024]{1,0:T(2,128)} %get-tuple-element.40), channel_id=1, source_target_pairs={{0,64},{64,128},{128,192},{192,0},{1,65},{65,129},{129,193},{193,1... | collective-permute-start | bytes 24584 | tf_op jit(solution)/shard_map/ppermute | solution.py:25
  11.3 8.9 %collective-permute-start.2 = (f32[2,1024]{1,0:T(2,128)}, f32[2,1024]{1,0:T(2,128)S(1)}, u32[]{:S(2)}, u32[]{:S(2)}) collective-permute-start(f32[2,1024]{1,0:T(2,128)} %get-tuple-element.40), channel_id=1, source_target_pairs={{0,192},{64,0},{128,64},{192,128},{1,193},{65,1},{129,65},{193,129... | collective-permute-start | bytes 24584 | tf_op jit(solution)/shard_map/ppermute | solution.py:25
  13.6 28.8 %collective-permute-start.6 = (bf16[2048,512]{1,0:T(8,128)(2,1)}, bf16[2048,512]{1,0:T(8,128)(2,1)}, u32[]{:S(2)}, u32[]{:S(2)}) collective-permute-start(bf16[2048,512]{1,0:T(8,128)(2,1)} %get-tuple-element.39), channel_id=1, source_target_pairs={{1,0},{2,1},{3,2},{4,3},{5,4},{6,5},{7,6},{8,7},{9,8},{10,9},{11,1... | collective-permute-start | bytes 6291464 | tf_op jit(solution)/shard_map/ppermute | solution.py:40
  17.0 30.2 %collective-permute-start.8 = (bf16[2048,512]{1,0:T(8,128)(2,1)S(1)}, bf16[2048,512]{1,0:T(8,128)(2,1)}, u32[]{:S(2)}, u32[]{:S(2)}) collective-permute-start(bf16[2048,512]{1,0:T(8,128)(2,1)S(1)} %get-tuple-element.41), channel_id=1, source_target_pairs={{0,1},{1,2},{2,3},{3,4},{4,5},{5,6},{6,7},{7,8},{8,9},{9,10},{10,1... | collective-permute-start | bytes 6291464 | tf_op jit(solution)/shard_map/ppermute | solution.py:35
  23.7 18.8 %collective-permute-start.7 = (f32[4,512]{1,0:T(4,128)S(1)}, f32[4,512]{1,0:T(4,128)S(1)}, u32[]{:S(2)}, u32[]{:S(2)}) collective-permute-start(f32[4,512]{1,0:T(4,128)S(1)} %get-tuple-element.73), channel_id=1, source_target_pairs={{1,0},{2,1},{3,2},{4,3},{5,4},{6,5},{7,6},{8,7},{9,8},{10,9},{11,1... | collective-permute-start | bytes 24584 | tf_op jit(solution)/shard_map/ppermute | solution.py:40
  26.3 20.9 %collective-permute-start.9 = (f32[4,512]{1,0:T(4,128)S(1)}, f32[4,512]{1,0:T(4,128)S(1)}, u32[]{:S(2)}, u32[]{:S(2)}) collective-permute-start(f32[4,512]{1,0:T(4,128)S(1)} %get-tuple-element.72), channel_id=1, source_target_pairs={{0,1},{1,2},{2,3},{3,4},{4,5},{5,6},{6,7},{7,8},{8,9},{9,10},{10,1... | collective-permute-start | bytes 24584 | tf_op jit(solution)/shard_map/ppermute | solution.py:35
  34.7 21.0 %collective-permute-start.3 = (s16[384,512]{1,0:T(8,128)(2,1)S(1)}, s16[384,512]{1,0:T(8,128)(2,1)S(1)}, u32[]{:S(2)}, u32[]{:S(2)}) collective-permute-start(s16[384,512]{1,0:T(8,128)(2,1)S(1)} %get-tuple-element.64), channel_id=1, source_target_pairs={{0,64},{64,128},{128,192},{192,0},{1,65},{65,129},{129,193},{193,1... | collective-permute-start | bytes 1179656 | tf_op jit(solution)/shard_map/ppermute | solution.py:25
  42.4 13.3 %collective-permute-start.4 = (s16[384,512]{1,0:T(8,128)(2,1)S(1)}, s16[384,512]{1,0:T(8,128)(2,1)S(1)}, u32[]{:S(2)}, u32[]{:S(2)}) collective-permute-start(s16[384,512]{1,0:T(8,128)(2,1)S(1)} %get-tuple-element.63), channel_id=1, source_target_pairs={{0,128},{64,192},{128,0},{192,64},{1,129},{65,193},{129,1},{193,65... | collective-permute-start | bytes 1179656 | tf_op jit(solution)/shard_map/ppermute | solution.py:25
  42.5 15.4 %collective-permute-start.5 = (s16[384,512]{1,0:T(8,128)(2,1)S(1)}, s16[384,512]{1,0:T(8,128)(2,1)S(1)}, u32[]{:S(2)}, u32[]{:S(2)}) collective-permute-start(s16[384,512]{1,0:T(8,128)(2,1)S(1)} %get-tuple-element.62), channel_id=1, source_target_pairs={{0,192},{64,0},{128,64},{192,128},{1,193},{65,1},{129,65},{193,129... | collective-permute-start | bytes 1179656 | tf_op jit(solution)/shard_map/ppermute | solution.py:25
  47.3 14.9 %copy-start = (s32[1024]{0:T(1024)S(1)}, s32[1024]{0:T(1024)}, u32[]{:S(2)}) copy-start(s32[1024]{0:T(1024)} %param.9) | copy-start | bytes 12292
  47.3 14.9 %copy-start.1 = (s32[1024]{0:T(1024)S(1)}, s32[1024]{0:T(1024)}, u32[]{:S(2)}) copy-start(s32[1024]{0:T(1024)} %param.10) | copy-start | bytes 12292
  50.4 11.0 %collective-permute-start.10 = (s16[136,512]{1,0:T(8,128)(2,1)S(1)}, s16[136,512]{1,0:T(8,128)(2,1)S(1)}, u32[]{:S(2)}, u32[]{:S(2)}) collective-permute-start(s16[136,512]{1,0:T(8,128)(2,1)S(1)} %get-tuple-element.68), channel_id=1, source_target_pairs={{0,64},{64,128},{128,192},{192,0},{1,65},{65,129},{129,193},{193,1... | collective-permute-start | bytes 417800 | tf_op jit(solution)/shard_map/ppermute | solution.py:25
  50.4 11.0 %collective-permute-start.11 = (s16[136,512]{1,0:T(8,128)(2,1)S(1)}, s16[136,512]{1,0:T(8,128)(2,1)S(1)}, u32[]{:S(2)}, u32[]{:S(2)}) collective-permute-start(s16[136,512]{1,0:T(8,128)(2,1)S(1)} %get-tuple-element.69), channel_id=1, source_target_pairs={{0,128},{64,192},{128,0},{192,64},{1,129},{65,193},{129,1},{193,65... | collective-permute-start | bytes 417800 | tf_op jit(solution)/shard_map/ppermute | solution.py:25
  55.7 6.4 %collective-permute-start.12 = (s16[136,512]{1,0:T(8,128)(2,1)S(1)}, s16[136,512]{1,0:T(8,128)(2,1)S(1)}, u32[]{:S(2)}, u32[]{:S(2)}) collective-permute-start(s16[136,512]{1,0:T(8,128)(2,1)S(1)} %get-tuple-element.66), channel_id=1, source_target_pairs={{0,192},{64,0},{128,64},{192,128},{1,193},{65,1},{129,65},{193,129... | collective-permute-start | bytes 417800 | tf_op jit(solution)/shard_map/ppermute | solution.py:25
  92.4 6.7 %collective-permute-start.16 = (f32[2,256]{1,0:T(2,128)S(1)}, f32[2,256]{1,0:T(2,128)S(1)}, u32[]{:S(2)}, u32[]{:S(2)}) collective-permute-start(f32[2,256]{1,0:T(2,128)S(1)} %get-tuple-element.70), channel_id=1, source_target_pairs={{0,128},{64,192},{128,0},{192,64},{1,129},{65,193},{129,1},{193,65... | collective-permute-start | bytes 6152 | tf_op jit(solution)/shard_map/ppermute | solution.py:25
  94.9 4.3 %collective-permute-start.17 = (f32[2,256]{1,0:T(2,128)S(1)}, f32[2,256]{1,0:T(2,128)S(1)}, u32[]{:S(2)}, u32[]{:S(2)}) collective-permute-start(f32[2,256]{1,0:T(2,128)S(1)} %get-tuple-element.70), channel_id=1, source_target_pairs={{0,64},{64,128},{128,192},{192,0},{1,65},{65,129},{129,193},{193,1... | collective-permute-start | bytes 6152 | tf_op jit(solution)/shard_map/ppermute | solution.py:25
  95.8 3.3 %collective-permute-start.18 = (f32[2,256]{1,0:T(2,128)S(1)}, f32[2,256]{1,0:T(2,128)S(1)}, u32[]{:S(2)}, u32[]{:S(2)}) collective-permute-start(f32[2,256]{1,0:T(2,128)S(1)} %get-tuple-element.70), channel_id=1, source_target_pairs={{0,192},{64,0},{128,64},{192,128},{1,193},{65,1},{129,65},{193,129... | collective-permute-start | bytes 6152 | tf_op jit(solution)/shard_map/ppermute | solution.py:25
  97.6 8.5 %collective-permute-start.13 = (f32[2,16384]{1,0:T(2,128)S(1)}, f32[2,16384]{1,0:T(2,128)S(1)}, u32[]{:S(2)}, u32[]{:S(2)}) collective-permute-start(f32[2,16384]{1,0:T(2,128)S(1)} %bitcast.66), channel_id=1, source_target_pairs={{0,192},{64,0},{128,64},{192,128},{1,193},{65,1},{129,65},{193,129... | collective-permute-start | bytes 393224 | tf_op jit(solution)/shard_map/ppermute | solution.py:25
  98.6 7.5 %collective-permute-start.14 = (f32[2,16384]{1,0:T(2,128)S(1)}, f32[2,16384]{1,0:T(2,128)S(1)}, u32[]{:S(2)}, u32[]{:S(2)}) collective-permute-start(f32[2,16384]{1,0:T(2,128)S(1)} %bitcast.67), channel_id=1, source_target_pairs={{0,128},{64,192},{128,0},{192,64},{1,129},{65,193},{129,1},{193,65... | collective-permute-start | bytes 393224 | tf_op jit(solution)/shard_map/ppermute | solution.py:25
  99.1 8.6 %collective-permute-start.15 = (f32[2,16384]{1,0:T(2,128)S(1)}, f32[2,16384]{1,0:T(2,128)S(1)}, u32[]{:S(2)}, u32[]{:S(2)}) collective-permute-start(f32[2,16384]{1,0:T(2,128)S(1)} %bitcast.68), channel_id=1, source_target_pairs={{0,64},{64,128},{128,192},{192,0},{1,65},{65,129},{129,193},{193,1... | collective-permute-start | bytes 393224 | tf_op jit(solution)/shard_map/ppermute | solution.py:25
  99.9 17.3 %all-to-all-start.1 = ((f32[64,2,256]{2,1,0:T(2,128)}), f32[64,2,256]{2,1,0:T(2,128)S(1)}, u32[]{:S(2)}, u32[]{:S(2)}) async-start(f32[64,2,256]{2,1,0:T(2,128)} %broadcast_in_dim.7), calls=%async_computation.1 | async-start | bytes 262144 | tf_op jit(solution)/shard_map/all_to_all | solution.py:15
  (1 other events, 14.8 us)
